TPU v7x, 32 devices: a 4x4x1 block of a 4x4x8 slice. The times are simulated.
32 devices in a mesh: dp: 1 (over z), tp2: 4 (over y), tp: 8 (over x, core).
Axes of the slice: x: 4, y: 4, z: 1, core: 2. Of those that a mesh axis runs over, the one named last changes fastest.
The devices are a block of a 4x4x8 slice.
Arguments:
- attn_out: bfloat16 [8192, 12288], P('dp', 'tp')
- w_out: bfloat16 [12288, 12288], P('tp', 'tp2')
- residual: bfloat16 [8192, 12288], P(('dp', 'tp'), 'tp2')
- norm_gain: float32 [12288], P('tp2')
Outputs:
- output 1: bfloat16 [8192, 12288], P(('dp', 'tp'), 'tp2')
- output 2: bfloat16 [8192, 12288], P(('dp', 'tp'), 'tp2')
All inputs are finite; a program needn't handle non-finite values.
Results may differ from a plain program's by a relative error of at most 0.00707124.
Values are sent between devices in bfloat16 or wider.
A program may use at most 768 MiB of HBM per device.

v0:
```python
import jax
import jax.numpy as jnp
from jax import lax
from jax.sharding import PartitionSpec as P, NamedSharding

EPS_NORM = 1e-6


def solution(mesh):
    tp_size = mesh.shape["tp"]
    col_groups = mesh.shape["tp2"]

    def local_step(attn_blk, w_blk, res_blk, gain_blk):
        block_prod = jnp.dot(attn_blk, w_blk, preferred_element_type=jnp.float32).astype(jnp.bfloat16)
        token_rows, local_cols = block_prod.shape
        received = lax.all_to_all(block_prod, "tp", 0, 0, tiled=True)
        y_sum = jnp.sum(received.reshape(tp_size, token_rows // tp_size, local_cols), axis=0, dtype=jnp.float32)
        hidden = res_blk.astype(jnp.float32) + y_sum
        sq_sum = lax.psum(jnp.sum(hidden * hidden, axis=-1, keepdims=True), "tp2")
        inv_rms = lax.rsqrt(sq_sum / (local_cols * col_groups) + EPS_NORM)
        normed = hidden * inv_rms * gain_blk
        return hidden.astype(jnp.bfloat16), normed.astype(jnp.bfloat16)

    row_spec = P(("dp", "tp"), "tp2")
    return jax.shard_map(local_step, mesh=mesh, in_specs=(P("dp", "tp"), P("tp", "tp2"), row_spec, P("tp2")), out_specs=(row_spec, row_spec), check_vma=False)
```

profile of v0, /device:TPU:96, one launch (start us, length us, event | category | flops | bytes accessed | tf_op | source)
XLA Modules:
  0.0 700.3 jit_solution(4791329086732315479)
XLA Ops:
  0.6 86.6 %convolution_convert_fusion = bf16[8192,3072]{1,0:T(8,128)(2,1)} fusion(bf16[8192,1536]{1,0:T(8,128)(2,1)} %param.4, bf16[1536,3072]{1,0:T(8,128)(2,1)} %param.5), kind=kOutput, calls=%fused_computation.1 | convolution fusion | flops 77334577152 | bytes 84934656 | tf_op jit(solution)/shard_map/dot_general | solution.py:14
  87.2 558.6 %all_to_all.9 = bf16[8,1024,3072]{2,1,0:T(8,128)(2,1)} all-to-all(bf16[8,1024,3072]{2,1,0:T(8,128)(2,1)} %bitcast.5), channel_id=1, replica_groups=mesh['dp'=1,'tp2'=4,'tp'=8] {'tp'}, dimensions={0} | all-to-all | bytes 100663296 | tf_op jit(solution)/shard_map/all_to_all | solution.py:16
  645.8 21.5 %convert_reduce_fusion = f32[1024,3072]{1,0:T(8,128)} fusion(bf16[8,1024,3072]{2,1,0:T(8,128)(2,1)} %all_to_all.9), kind=kLoop, calls=%fused_computation | loop fusion | flops 47185920 | bytes 62914560 | tf_op jit(solution)/shard_map/reduce_sum | solution.py:17
  667.3 0.0 copy-start
  667.3 8.1 %multiply_reduce_fusion = f32[1024]{0:T(1024)S(1)} fusion(f32[1024,3072]{1,0:T(8,128)} %convert_reduce_fusion, bf16[1024,3072]{1,0:T(8,128)(2,1)} %param.6), kind=kLoop, calls=%fused_computation.3 | loop fusion | flops 12581888 | bytes 18878464 | tf_op jit(solution)/shard_map/reduce_sum | solution.py:19
  675.4 11.8 %psum.7 = f32[1024,1]{0,1:T(1,128)S(1)} all-reduce(f32[1024,1]{0,1:T(1,128)S(1)} %bitcast.7), channel_id=1, replica_groups=mesh['dp'=1,'tp2'=4,'tp'=8] {'tp2'}, use_global_device_ids=true, to_apply=%region_2.0 | all-reduce | flops 1024 | bytes 8192 | tf_op jit(solution)/shard_map/psum | solution.py:19
  687.2 0.0 copy-done
  687.2 13.1 %multiply_convert_fusion = (bf16[1024,3072]{1,0:T(8,128)(2,1)}, bf16[1024,3072]{1,0:T(8,128)(2,1)}) fusion(f32[3072]{0:T(1024)S(1)} %copy-done, f32[1024]{0:T(1024)S(1)} %bitcast.6, f32[1024,3072]{1,0:T(8,128)} %convert_reduce_fusion, bf16[1024,3072]{1,0:T(8,128)(2,1)} %param.6), kind=kLoop, calls=%fused_computation.2 | loop fusion | flops 18874368 | bytes 31473664 | tf_op jit(solution)/shard_map/convert_element_type | solution.py:22
  (1 shorter events, 0.0 us)
Async XLA Ops:
  667.3 19.9 %copy-start = (f32[3072]{0:T(1024)S(1)}, f32[3072]{0:T(1024)}, u32[]{:S(2)}) copy-start(f32[3072]{0:T(1024)} %param.7) | copy-start | bytes 36868
where the time goes:
time: 701 us; the launch traced here: 700 us
  blocking collectives  570 us (81%)
  matrix products  86.6 us (12%)
  other arithmetic  42.7 us (6%)
    all_to_all x1, blocking collectives, local_step(): received = lax.all_to_all(block_prod, 'tp', 0, 0, tiled=True)  559 us
    dot_general x1, matrix products, local_step(): jnp.dot(attn_blk, w_blk, preferred_element_type=jnp.float32)  86.6 us
    reduce_sum x1, other arithmetic, local_step(): jnp.sum(received.reshape(tp_size, token_rows // tp_size, local_cols), axi...  21.5 us

commit v1 on v0

v1 whole, which is shorter than its diff:
```python
import functools

import jax
import jax.numpy as jnp
from jax import lax
from jax.experimental import pallas as pl
from jax.experimental.pallas import tpu as pltpu
from jax.sharding import PartitionSpec as P

EPS_NORM = 1e-6
MESH = pl.DeviceIdType.MESH
CORES = 2
CN = 256
WS = 3
LAG = 2
AHEAD = 3


def kernel(ny, chips, a, w, r, h_out, ssq_out, wbuf, av, wv, ov, rbuf, lv, rv, hv, ssacc, svr,
           al_sem, ap_send, ap_recv, ax_send, ax_recv, ay_send, ay_recv, af_send, af_recv,
           wp_send, wp_recv, wa_send, wa_recv, wf_send, wf_recv, o_send, o_recv,
           wl_sem, r_sem, h_sem, s_send, s_recv):
    rows, cols = r.shape
    chunks = cols // CN
    quarter = rows // ny
    tile = min(256, rows)
    me, y = lax.axis_index("tp"), lax.axis_index("tp2")
    x, c = lax.div(me, CORES), lax.rem(me, CORES)
    o = 1 - c
    xa = x + 1 - 2 * lax.rem(x, 2)
    xb = chips - 1 - x
    xab = chips - 1 - xa
    yp, ym = lax.rem(y + 1, ny), lax.rem(y + ny - 1, ny)
    part = {"tp": x * CORES + o}
    acore, aother = {"tp": xa * CORES + c}, {"tp": xa * CORES + o}
    bcore = {"tp": xb * CORES + c}
    up, down = {"tp2": yp}, {"tp2": ym}

    def remote(src, dst, send, recv, device):
        return pltpu.make_async_remote_copy(
            src_ref=src, dst_ref=dst, send_sem=send, recv_sem=recv, device_id=device, device_id_type=MESH)

    def arow(owner, size=None, shift=0):
        return pl.ds(pl.multiple_of(owner * rows + shift, 16), rows if size is None else size)

    def qrow(q):
        return pl.ds(pl.multiple_of(q * quarter, 16), quarter)

    def wcol(j):
        return pl.ds(pl.multiple_of(j * CN, CN), CN)

    own_rows = (xb * CORES + c, me)
    part_rows = (xb * CORES + o, x * CORES + o)

    def a_local(g):
        return pltpu.make_async_copy(a.at[arow(own_rows[g])], av.at[g, 0], al_sem.at[g])

    def a_part(g):
        return remote(a.at[arow(part_rows[g])], av.at[g, 1], ap_send.at[g], ap_recv.at[g], part)

    def a_cross(g, s):
        core, device = ((c, acore), (o, aother))[s]
        owner = (xab, xa)[g] * CORES + core
        return remote(a.at[arow(owner, quarter, y * quarter)], av.at[g, 2 + s, qrow(y)],
                      ax_send.at[g, s], ax_recv.at[g, s], device)

    def a_near(g, s, d):
        ref = av.at[g, 2 + s, qrow(y)]
        return remote(ref, ref, ay_send.at[g, s, d], ay_recv.at[g, s, d], (up, down)[d])

    def a_far(g, s):
        ref = av.at[g, 2 + s, qrow((ym, yp)[s])]
        return remote(ref, ref, af_send.at[g, s], af_recv.at[g, s], (up, down)[s])

    def a_first(g):
        for s in range(2):
            a_cross(g, s).wait_recv()
            for d in range(2):
                a_near(g, s, d).start()

    def a_second(g):
        for s in range(2):
            a_near(g, s, s).wait_recv()
            a_far(g, s).start()

    def a_third(g):
        a_local(g).wait()
        a_part(g).wait_recv()
        for s in range(2):
            a_near(g, s, 1 - s).wait_recv()
            a_far(g, s).wait_recv()

    def w_part(j):
        return remote(w.at[:, wcol(j)], wbuf.at[0, j], wp_send.at[j], wp_recv.at[j], part)

    def w_cross(j):
        return remote(w.at[:, wcol(j)], wbuf.at[1, j], wa_send.at[j], wa_recv.at[j], acore)

    def w_pass(j):
        return remote(wbuf.at[1, j], wbuf.at[2, j], wf_send.at[j], wf_recv.at[j], part)

    def w_load(j, k):
        src = w.at[:, wcol(j)] if k == 0 else wbuf.at[k - 1, j]
        return pltpu.make_async_copy(src, wv.at[lax.rem(j, WS), k], wl_sem.at[k])

    def out_copy(j):
        slot = lax.rem(j, 2)
        return remote(ov.at[slot], rbuf.at[j], o_send.at[slot], o_recv.at[j], bcore)

    def r_load(j):
        return pltpu.make_async_copy(r.at[:, wcol(j)], rv, r_sem)

    def h_store(j):
        slot = lax.rem(j, 2)
        return pltpu.make_async_copy(hv.at[slot], h_out.at[:, wcol(j)], h_sem.at[slot])

    def gemm(g, j, dst):
        slot = lax.rem(j, WS)

        def step(i, carry):
            rs = pl.ds(pl.multiple_of(i * tile, tile), tile)
            acc = None
            for k in range(4):
                prod = jnp.dot(av[g, k, rs, :], wv[slot, k], preferred_element_type=jnp.float32)
                prod = prod.astype(jnp.bfloat16).astype(jnp.float32)
                acc = prod if acc is None else acc + prod
            dst[rs, :] = acc
            return carry

        lax.fori_loop(0, rows // tile, step, 0)

    barrier = pltpu.get_barrier_semaphore()
    peers = [part, acore, aother, bcore] + [{"tp2": lax.rem(y + d, ny)} for d in range(1, ny)]
    for peer in peers:
        pl.semaphore_signal(barrier, inc=1, device_id=peer, device_id_type=MESH)
    pl.semaphore_wait(barrier, len(peers))

    for s in range(2):
        a_cross(0, s).start()
    a_part(0).start()
    w_cross(0).start()
    w_part(0).start()
    w_cross(1).start()
    w_part(1).start()
    for s in range(2):
        a_cross(1, s).start()
    a_part(1).start()
    for j in range(2, AHEAD):
        w_cross(j).start()
        w_part(j).start()
    a_local(0).start()
    a_local(1).start()
    ssacc[...] = jnp.zeros_like(ssacc)
    a_first(0)
    a_second(0)
    a_third(0)

    def step(j, carry):
        @pl.when(j < chunks)
        def _():
            w_cross(j).wait_recv()
            w_pass(j).start()

            @pl.when(j + AHEAD < chunks)
            def _():
                w_cross(j + AHEAD).start()
                w_part(j + AHEAD).start()

            w_load(j, 0).start()
            w_load(j, 2).start()
            w_part(j).wait_recv()
            w_load(j, 1).start()
            w_pass(j).wait_recv()
            w_load(j, 3).start()

            @pl.when(j >= 2)
            def _():
                out_copy(j - 2).wait_send()

            for k in range(4):
                w_load(j, k).wait()
            gemm(0, j, ov.at[lax.rem(j, 2)])

        @pl.when(j == 1)
        def _():
            a_first(1)

        @pl.when(j == 2)
        def _():
            a_second(1)
            a_third(1)

        @pl.when(j >= LAG)
        def _():
            r_load(j - LAG).start()

        @pl.when(j < chunks)
        def _():
            out_copy(j).start()

        @pl.when(j >= LAG)
        def _():
            i = j - LAG
            gemm(1, i, lv)
            r_load(i).wait()
            slot = lax.rem(i, 2)

            @pl.when(i >= 2)
            def _():
                h_store(i - 2).wait()

            out_copy(i).wait_recv()

            def merge(t, carry):
                rs = pl.ds(pl.multiple_of(t * 64, 64), 64)
                h = rv[rs, :].astype(jnp.float32) + (lv[rs, :] + rbuf[i, rs, :])
                hv[slot, rs, :] = h
                sq = h * h
                acc = ssacc[rs, :]
                for l in range(CN // 128):
                    acc = acc + sq[:, l * 128:(l + 1) * 128]
                ssacc[rs, :] = acc
                return carry

            lax.fori_loop(0, rows // 64, merge, 0)
            h_store(i).start()

        return carry

    lax.fori_loop(0, chunks + LAG, step, 0)

    svr[y] = lax.dot_general(jnp.ones((8, 128), jnp.float32), ssacc[...], (((1,), (1,)), ((), ())),
                             preferred_element_type=jnp.float32, precision=lax.Precision.HIGHEST)
    h_store(chunks - 2).wait()
    h_store(chunks - 1).wait()
    sums = [remote(svr.at[y], svr.at[y], s_send.at[d - 1], s_recv.at[d - 1], {"tp2": lax.rem(y + d, ny)})
            for d in range(1, ny)]
    for copy in sums:
        copy.start()

    def drain(j, carry):
        w_cross(j).wait_send()
        w_part(j).wait_send()
        w_pass(j).wait_send()
        return carry

    lax.fori_loop(0, chunks, drain, 0)
    for g in range(2):
        a_part(g).wait_send()
        for s in range(2):
            a_cross(g, s).wait_send()
            a_far(g, s).wait_send()
            for d in range(2):
                a_near(g, s, d).wait_send()
    out_copy(chunks - 2).wait_send()
    out_copy(chunks - 1).wait_send()
    for d in range(1, ny):
        src = lax.rem(y + ny - d, ny)
        remote(svr.at[src], svr.at[src], s_send.at[d - 1], s_recv.at[d - 1], part).wait_recv()
    total = svr[0]
    for q in range(1, ny):
        total = total + svr[q]
    ssq_out[...] = total
    for copy in sums:
        copy.wait_send()


def solution(mesh):
    tp, ny = mesh.shape["tp"], mesh.shape["tp2"]
    chips = tp // CORES

    def local_step(a, w, r, gain):
        depth, cols = w.shape
        rows = r.shape[0]
        chunks = cols // CN
        dma = pltpu.SemaphoreType.DMA
        any_space = pl.BlockSpec(memory_space=pl.ANY)
        hidden, ssq, _ = pl.pallas_call(
            functools.partial(kernel, ny, chips),
            out_shape=(
                jax.ShapeDtypeStruct((rows, cols), jnp.float32),
                jax.ShapeDtypeStruct((8, rows), jnp.float32),
                jax.ShapeDtypeStruct((3, chunks, depth, CN), jnp.bfloat16),
            ),
            in_specs=[any_space] * 3,
            out_specs=(any_space, pl.BlockSpec(memory_space=pltpu.VMEM), any_space),
            scratch_shapes=[
                pltpu.VMEM((2, 4, rows, depth), jnp.bfloat16),
                pltpu.VMEM((WS, 4, depth, CN), jnp.bfloat16),
                pltpu.VMEM((2, rows, CN), jnp.float32),
                pltpu.VMEM((chunks, rows, CN), jnp.float32),
                pltpu.VMEM((rows, CN), jnp.float32),
                pltpu.VMEM((rows, CN), jnp.bfloat16),
                pltpu.VMEM((2, rows, CN), jnp.float32),
                pltpu.VMEM((rows, 128), jnp.float32),
                pltpu.VMEM((ny, 8, rows), jnp.float32),
                dma((2,)), dma((2,)), dma((2,)), dma((2, 2)), dma((2, 2)),
                dma((2, 2, 2)), dma((2, 2, 2)), dma((2, 2)), dma((2, 2)),
                dma((chunks,)), dma((chunks,)), dma((chunks,)), dma((chunks,)), dma((chunks,)), dma((chunks,)),
                dma((2,)), dma((chunks,)),
                dma((4,)), dma(()), dma((2,)), dma((ny - 1,)), dma((ny - 1,)),
            ],
            compiler_params=pltpu.CompilerParams(
                collective_id=0, has_side_effects=True, vmem_limit_bytes=67043328),
            cost_estimate=pl.CostEstimate(
                flops=2 * 8 * rows * depth * cols, bytes_accessed=8 * depth * cols * 2, transcendentals=0),
        )(a, w, r)
        inv_rms = lax.rsqrt(ssq[0] / (cols * ny) + EPS_NORM)
        normed = hidden * inv_rms[:, None] * gain
        return hidden.astype(jnp.bfloat16), normed.astype(jnp.bfloat16)

    row_spec = P(("dp", "tp"), "tp2")
    return jax.shard_map(local_step, mesh=mesh, in_specs=(P("dp", "tp"), P("tp", "tp2"), row_spec, P("tp2")),
                         out_specs=(row_spec, row_spec), check_vma=False)
```

time: 701 us -> 405 us (0.58)
  blocking collectives: 570 us -> 0 us
  Pallas kernels: 0 us -> 386 us
  matrix products: 86.6 us -> 0 us
  other arithmetic: 42.7 us -> 17.1 us
    all_to_all x1 -> x0, blocking collectives: 559 us -> none  [local_step(): received = lax.all_to_all(block_prod, 'tp', 0, 0, tiled=True)]
    pallas_call x0 -> x1, Pallas kernels: none -> 386 us  [local_step(): pl.pallas_call(functools.partial(kernel, ny, chips), out_shape=(jax.Shape...]
    dot_general x1 -> x0, matrix products: 86.6 us -> none  [local_step(): jnp.dot(attn_blk, w_blk, preferred_element_type=jnp.float32)]
    reduce_sum x2 -> x0, other arithmetic: 29.6 us -> none  [the longest x1 21.5 us: local_step(): jnp.sum(received.reshape(tp_size, token_rows // tp_size, local_cols), axi...]
    psum x1 -> x0, blocking collectives: 11.8 us -> none  [local_step(): sq_sum = lax.psum(jnp.sum(hidden * hidden, axis=-1, keepdims=True), 'tp2')]
where the time goes in v1:
time: 405 us; the launch traced here: 404 us
  Pallas kernels  386 us (95%)
  other arithmetic  17.1 us (4%)
    pallas_call x1, Pallas kernels, local_step(): pl.pallas_call(functools.partial(kernel, ny, chips), out_shape=(jax.Shape...  386 us
    convert_element_type x1, other arithmetic, local_step(): return (hidden.astype(jnp.bfloat16), normed.astype(jnp.bfloat16))  16.3 us

profile of v1, /device:TPU:96, one launch (start us, length us, event | category | flops | bytes accessed | tf_op | source)
XLA Modules:
  0.0 403.7 jit_solution(7565204271061896728)
XLA Ops:
  0.6 386.0 %shard_map.59 = (f32[1024,3072]{1,0:T(8,128)}, f32[8,1024]{1,0:T(8,128)}, bf16[3,12,1536,256]{3,2,1,0:T(8,128)(2,1)}) custom-call(bf16[8192,1536]{1,0:T(8,128)(2,1)} %a.1, bf16[1536,3072]{1,0:T(8,128)(2,1)} %w.1, bf16[1024,3072]{1,0:T(8,128)(2,1)} %r.1), custom_call_target="tpu_custom_call" | custom-call | flops 77309411328 | bytes 75497472 | tf_op jit(solution)/shard_map/pallas_call | solution.py:278
  386.6 0.8 add_rsqrt_fusion
  387.4 16.3 %multiply_convert_fusion = (bf16[1024,3072]{1,0:T(8,128)(2,1)}, bf16[1024,3072]{1,0:T(8,128)(2,1)}) fusion(f32[1024,3072]{1,0:T(8,128)} %get-tuple-element.4, f32[3072]{0:T(1024)} %param.7, f32[1024]{0:T(1024)S(1)} %bitcast.1), kind=kLoop, calls=%fused_computation | loop fusion | flops 12582912 | bytes 25182208 | tf_op jit(solution)/shard_map/convert_element_type | solution.py:310

commit v2 on v1

v2 whole, which is shorter than its diff:
```python
import functools

import jax
import jax.numpy as jnp
from jax import lax
from jax.experimental import pallas as pl
from jax.experimental.pallas import tpu as pltpu
from jax.sharding import PartitionSpec as P

EPS_NORM = 1e-6
MESH = pl.DeviceIdType.MESH
CORES = 2
CN = 256
LAG = 6
AHEAD = 6
PIECES = 4


def kernel(ny, chips, a, w, r, h_out, ssq_out, wbuf, av, wv, ov, rbuf, lv, rv, hv, ssacc, svr,
           at, pv, sb, sp, sf, sg,
           al_sem, ap_send, ap_recv, ax_send, ax_recv, ay_send, ay_recv, af_send, af_recv,
           wp_send, wp_recv, wa_send, wa_recv, wf_send, wf_recv, o_send, o_recv,
           wl_sem, r_sem, h_sem, s_send, s_recv, at_sem, sb_send, sb_recv, sp_send, sp_recv, sf_send, sf_recv):
    rows, cols = r.shape
    last = cols // CN - 1
    quarter = rows // ny
    piece = quarter // PIECES
    tile = min(256, rows)
    me, y = lax.axis_index("tp"), lax.axis_index("tp2")
    x, c = lax.div(me, CORES), lax.rem(me, CORES)
    o = 1 - c
    xa = x + 1 - 2 * lax.rem(x, 2)
    xb = chips - 1 - x
    xab = chips - 1 - xa
    yp, ym = lax.rem(y + 1, ny), lax.rem(y + ny - 1, ny)
    part = {"tp": x * CORES + o}
    acore, aother = {"tp": xa * CORES + c}, {"tp": xa * CORES + o}
    bcore, bother = {"tp": xb * CORES + c}, {"tp": xb * CORES + o}
    up, down = {"tp2": yp}, {"tp2": ym}

    def remote(src, dst, send, recv, device):
        return pltpu.make_async_remote_copy(
            src_ref=src, dst_ref=dst, send_sem=send, recv_sem=recv, device_id=device, device_id_type=MESH)

    def arow(owner, size=None, shift=0):
        return pl.ds(pl.multiple_of(owner * rows + shift, 16), rows if size is None else size)

    def qrow(q, t):
        return pl.ds(pl.multiple_of(q * quarter + t * piece, 16), piece)

    def wcol(j):
        return pl.ds(pl.multiple_of(j * CN, CN), CN)

    own_rows = (xb * CORES + c, me)
    part_rows = (xb * CORES + o, x * CORES + o)

    def a_local(g):
        return pltpu.make_async_copy(a.at[arow(own_rows[g])], av.at[g, 0], al_sem.at[g])

    def a_part(g):
        return remote(a.at[arow(part_rows[g])], av.at[g, 1], ap_send.at[g], ap_recv.at[g], part)

    def a_cross(g, s, t):
        core, device = ((c, acore), (o, aother))[s]
        owner = (xab, xa)[g] * CORES + core
        return remote(a.at[arow(owner, piece, y * quarter + t * piece)], av.at[g, 2 + s, qrow(y, t)],
                      ax_send.at[g, s, t], ax_recv.at[g, s, t], device)

    def a_near(g, s, t, d):
        ref = av.at[g, 2 + s, qrow(y, t)]
        return remote(ref, ref, ay_send.at[g, s, t, d], ay_recv.at[g, s, t, d], (up, down)[d])

    def a_far(g, s, t):
        ref = av.at[g, 2 + s, qrow((ym, yp)[s], t)]
        return remote(ref, ref, af_send.at[g, s, t], af_recv.at[g, s, t], (up, down)[s])

    def a_send(g, s):
        for t in range(PIECES):
            a_cross(g, s, t).start()

    def a_first(g, s, t):
        a_cross(g, s, t).wait_recv()
        for d in range(2):
            a_near(g, s, t, d).start()

    def a_second(g, s, t):
        a_near(g, s, t, s).wait_recv()
        a_far(g, s, t).start()

    def a_third(g):
        a_local(g).wait()
        a_part(g).wait_recv()
        for t in range(PIECES):
            for s in range(2):
                a_near(g, s, t, 1 - s).wait_recv()
                a_far(g, s, t).wait_recv()

    def w_part(j):
        return remote(w.at[:, wcol(j)], wbuf.at[0, j], wp_send.at[j], wp_recv.at[j], part)

    def w_cross(j):
        return remote(w.at[:, wcol(j)], wbuf.at[1, j], wa_send.at[j], wa_recv.at[j], acore)

    def w_pass(j):
        return remote(wbuf.at[1, j], wbuf.at[2, j], wf_send.at[j], wf_recv.at[j], part)

    def w_load(g, j, k):
        src = w.at[:, wcol(j)] if k == 0 else wbuf.at[k - 1, j]
        return pltpu.make_async_copy(src, wv.at[g, k], wl_sem.at[g, k])

    def out_copy(j):
        slot = lax.rem(j, 2)
        return remote(ov.at[slot], rbuf.at[j], o_send.at[slot], o_recv.at[j], bcore)

    def r_load(j):
        return pltpu.make_async_copy(r.at[:, wcol(j)], rv, r_sem)

    def h_store(j):
        return pltpu.make_async_copy(hv, h_out.at[:, wcol(j)], h_sem)

    def block_product(lhs, rhs):
        return jnp.dot(lhs, rhs, preferred_element_type=jnp.float32).astype(jnp.bfloat16)

    def gemm(g, dst):
        def step(i, carry):
            rs = pl.ds(pl.multiple_of(i * tile, tile), tile)
            acc = None
            for k in range(4):
                prod = block_product(av[g, k, rs, :], wv[g, k]).astype(jnp.float32)
                acc = prod if acc is None else acc + prod
            dst[rs, :] = acc
            return carry

        lax.fori_loop(0, rows // tile, step, 0)

    items = ((xb, 0), (xb, 1), (xab, 0), (xab, 1), (x, o), (xa, o), (x, c), (xa, c))

    def at_load(n):
        pos, core = items[n]
        return pltpu.make_async_copy(a.at[arow(pos * CORES + core)], at.at[n % 2], at_sem.at[n % 2])

    def item_send(n):
        if n < 4:
            slot = n // 2 * 2 + c
            device = {"tp": xb * CORES + n % 2}
            return remote(pv.at[n], sb.at[slot], sb_send.at[n], sb_recv.at[slot], device)
        return remote(pv.at[n], sp.at[n - 4], sp_send.at[n - 4], sp_recv.at[n - 4], part)

    def item(n):
        at_load(n).wait()

        def step(i, carry):
            rs = pl.ds(pl.multiple_of(i * tile, tile), tile)
            pv[n, rs, :] = block_product(at[n % 2, rs, :], wv[0, 0])
            return carry

        lax.fori_loop(0, rows // tile, step, 0)
        if n + 2 < len(items):
            at_load(n + 2).start()

    def sb_arrival(slot):
        return remote(pv.at[0], sb.at[slot], sb_send.at[0], sb_recv.at[slot], bcore)

    def sf_copy():
        return remote(sg, sf, sf_send, sf_recv, acore)

    def for_rows(body):
        def step(t, carry):
            body(pl.ds(pl.multiple_of(t * 64, 64), 64))
            return carry

        lax.fori_loop(0, rows // 64, step, 0)

    def finish(rs, h):
        hv[rs, :] = h
        sq = h * h
        acc = ssacc[rs, :]
        for l in range(CN // 128):
            acc = acc + sq[:, l * 128:(l + 1) * 128]
        ssacc[rs, :] = acc

    def wide(v):
        return v.astype(jnp.float32)

    barrier = pltpu.get_barrier_semaphore()
    peers = [part, acore, aother, bcore, bother] + [{"tp2": lax.rem(y + d, ny)} for d in range(1, ny)]
    for peer in peers:
        pl.semaphore_signal(barrier, inc=1, device_id=peer, device_id_type=MESH)
    w_last = pltpu.make_async_copy(w.at[:, wcol(last)], wv.at[0, 0], wl_sem.at[0, 0])
    w_last.start()
    at_load(0).start()
    at_load(1).start()
    pl.semaphore_wait(barrier, len(peers))

    for t in range(PIECES):
        for s in range(2):
            a_cross(0, s, t).start()
    a_part(0).start()
    for j in range(AHEAD):
        w_cross(j).start()
        w_part(j).start()
        if j == 3:
            a_send(1, 0)
        if j == 4:
            a_send(1, 1)
    a_part(1).start()
    w_last.wait()
    with jax.named_scope("items"):
        item(0)
        item(1)
        item_send(0).start()
        item(2)
        item_send(1).start()
        item(3)
        item_send(2).start()
    a_local(0).start()
    a_local(1).start()
    ssacc[...] = jnp.zeros_like(ssacc)
    item_send(3).start()
    with jax.named_scope("a0_first"):
        for t in range(PIECES):
            for s in range(2):
                a_first(0, s, t)
    with jax.named_scope("items_2"):
        for n in range(4, 8):
            item(n)
        item_send(4).start()
        item_send(5).start()
    with jax.named_scope("a0_second"):
        for t in range(PIECES):
            for s in range(2):
                a_second(0, s, t)
    with jax.named_scope("a0_third"):
        a_third(0)

    def merge_last(before):
        r_load(before + 1).wait()
        h_store(before).wait()
        r_load(last).start()
        sb_arrival(0).wait_recv()
        sb_arrival(1).wait_recv()
        with jax.named_scope("sf_wait"):
            sf_copy().wait_recv()
        r_load(last).wait()
        for_rows(lambda rs: finish(rs, wide(rv[rs, :]) + (
            (wide(pv[6, rs, :]) + wide(sp[0, rs, :])) + (wide(sb[0, rs, :]) + wide(sb[1, rs, :])) + sf[rs, :])))
        h_store(last).start()
        r_load(before + 1).start()

    def sum_last():
        for n in range(2):
            item_send(4 + n).wait_recv()
            sb_arrival(2 + n).wait_recv()

        def body(rs):
            sg[rs, :] = (wide(pv[7, rs, :]) + wide(sp[1, rs, :])) + (wide(sb[2, rs, :]) + wide(sb[3, rs, :]))

        for_rows(body)

    def step(j, carry):
        @pl.when(j < last)
        def _():
            with jax.named_scope("w_cross_wait"):
                w_cross(j).wait_recv()
            w_pass(j).start()

            @pl.when(j + AHEAD < last)
            def _():
                w_cross(j + AHEAD).start()
                w_part(j + AHEAD).start()

            w_load(0, j, 0).start()
            w_load(0, j, 2).start()
            with jax.named_scope("w_pass_wait"):
                w_part(j).wait_recv()
                w_load(0, j, 1).start()
                w_pass(j).wait_recv()
                w_load(0, j, 3).start()

            @pl.when(j >= 2)
            def _():
                with jax.named_scope("o_send_wait"):
                    out_copy(j - 2).wait_send()

            with jax.named_scope("w_load_wait"):
                for k in range(4):
                    w_load(0, j, k).wait()
            with jax.named_scope("gemm0"):
                gemm(0, ov.at[lax.rem(j, 2)])

        @pl.when(j >= LAG)
        def _():
            for k in range(4):
                w_load(1, j - LAG, k).start()
            r_load(j - LAG).start()

        @pl.when(j < last)
        def _():
            out_copy(j).start()

        @pl.when(j == 4)
        def _():
            with jax.named_scope("a1_4"):
                for t in range(PIECES):
                    a_first(1, 0, t)

        @pl.when(j == 5)
        def _():
            with jax.named_scope("a1_5"):
                for t in range(PIECES):
                    a_first(1, 1, t)
                for t in range(PIECES):
                    a_second(1, 0, t)

        @pl.when(j == LAG)
        def _():
            with jax.named_scope("a1_6"):
                for t in range(PIECES):
                    a_second(1, 1, t)
                a_third(1)

        @pl.when(j == last - 3)
        def _():
            with jax.named_scope("sum_last"):
                sum_last()

        @pl.when(j == last + 1)
        def _():
            with jax.named_scope("merge_last"):
                merge_last(j - LAG - 1)

        @pl.when(j >= LAG)
        def _():
            i = j - LAG
            with jax.named_scope("local_load_wait"):
                for k in range(4):
                    w_load(1, i, k).wait()
                r_load(i).wait()
            with jax.named_scope("gemm1"):
                gemm(1, lv)

            @pl.when(i >= 1)
            def _():
                h_store(i - 1).wait()

            with jax.named_scope("o_recv_wait"):
                out_copy(i).wait_recv()
            with jax.named_scope("merge"):
                for_rows(lambda rs: finish(rs, wide(rv[rs, :]) + (lv[rs, :] + rbuf[i, rs, :])))
            h_store(i).start()

        @pl.when(j == last - 3)
        def _():
            sf_copy().start()

        return carry

    lax.fori_loop(0, last + LAG, step, 0)

    svr[y] = lax.dot_general(jnp.ones((8, 128), jnp.float32), ssacc[...], (((1,), (1,)), ((), ())),
                             preferred_element_type=jnp.float32, precision=lax.Precision.HIGHEST)

    def drain(j, carry):
        w_cross(j).wait_send()
        w_part(j).wait_send()
        w_pass(j).wait_send()
        return carry

    lax.fori_loop(0, last, drain, 0)
    for g in range(2):
        a_part(g).wait_send()
        for s in range(2):
            for t in range(PIECES):
                a_cross(g, s, t).wait_send()
                a_far(g, s, t).wait_send()
                for d in range(2):
                    a_near(g, s, t, d).wait_send()
    for n in range(6):
        item_send(n).wait_send()
    sf_copy().wait_send()
    sums = [remote(svr.at[y], svr.at[y], s_send.at[d - 1], s_recv.at[d - 1], {"tp2": lax.rem(y + d, ny)})
            for d in range(1, ny)]
    for copy in sums:
        copy.start()
    out_copy(last - 2).wait_send()
    out_copy(last - 1).wait_send()
    h_store(last - 1).wait()
    for d in range(1, ny):
        src = lax.rem(y + ny - d, ny)
        remote(svr.at[src], svr.at[src], s_send.at[d - 1], s_recv.at[d - 1], part).wait_recv()
    total = svr[0]
    for q in range(1, ny):
        total = total + svr[q]
    ssq_out[...] = total
    for copy in sums:
        copy.wait_send()


def norm_kernel(width, h, ssq, gain, hidden, normed):
    inv_rms = lax.rsqrt(ssq[...] / width + EPS_NORM)
    scale = jnp.transpose(inv_rms)[:, :1]
    value = h[...]
    hidden[...] = value.astype(jnp.bfloat16)
    normed[...] = (value * scale * gain[...]).astype(jnp.bfloat16)


def solution(mesh):
    tp, ny = mesh.shape["tp"], mesh.shape["tp2"]
    chips = tp // CORES

    def local_step(a, w, r, gain):
        depth, cols = w.shape
        rows = r.shape[0]
        last = cols // CN - 1
        dma = pltpu.SemaphoreType.DMA
        any_space = pl.BlockSpec(memory_space=pl.ANY)
        bf16, f32 = jnp.bfloat16, jnp.float32
        h, ssq, _ = pl.pallas_call(
            functools.partial(kernel, ny, chips),
            out_shape=(
                jax.ShapeDtypeStruct((rows, cols), f32),
                jax.ShapeDtypeStruct((8, rows), f32),
                jax.ShapeDtypeStruct((3, last, depth, CN), bf16),
            ),
            in_specs=[any_space] * 3,
            out_specs=(any_space, pl.BlockSpec(memory_space=pltpu.VMEM), any_space),
            scratch_shapes=[
                pltpu.VMEM((2, 4, rows, depth), bf16),
                pltpu.VMEM((2, 4, depth, CN), bf16),
                pltpu.VMEM((2, rows, CN), f32),
                pltpu.VMEM((last, rows, CN), f32),
                pltpu.VMEM((rows, CN), f32),
                pltpu.VMEM((rows, CN), bf16),
                pltpu.VMEM((rows, CN), f32),
                pltpu.VMEM((rows, 128), f32),
                pltpu.VMEM((ny, 8, rows), f32),
                pltpu.VMEM((2, rows, depth), bf16),
                pltpu.VMEM((8, rows, CN), bf16),
                pltpu.VMEM((4, rows, CN), bf16),
                pltpu.VMEM((2, rows, CN), bf16),
                pltpu.VMEM((rows, CN), f32),
                pltpu.VMEM((rows, CN), f32),
                dma((2,)), dma((2,)), dma((2,)), dma((2, 2, PIECES)), dma((2, 2, PIECES)),
                dma((2, 2, PIECES, 2)), dma((2, 2, PIECES, 2)), dma((2, 2, PIECES)), dma((2, 2, PIECES)),
                dma((last,)), dma((last,)), dma((last,)), dma((last,)), dma((last,)), dma((last,)),
                dma((2,)), dma((last,)),
                dma((2, 4)), dma(()), dma(()), dma((ny - 1,)), dma((ny - 1,)),
                dma((2,)), dma((4,)), dma((4,)), dma((2,)), dma((2,)), dma(()), dma(()),
            ],
            compiler_params=pltpu.CompilerParams(
                collective_id=0, has_side_effects=True, vmem_limit_bytes=67043328),
            cost_estimate=pl.CostEstimate(
                flops=2 * 8 * rows * depth * cols, bytes_accessed=8 * depth * cols * 2, transcendentals=0),
        )(a, w, r)
        span = 128
        row_block = pl.BlockSpec((span, cols), lambda i: (i, 0))
        return pl.pallas_call(
            functools.partial(norm_kernel, cols * ny),
            grid=(rows // span,),
            out_shape=(jax.ShapeDtypeStruct((rows, cols), bf16),) * 2,
            in_specs=[row_block, pl.BlockSpec((8, span), lambda i: (0, i)), pl.BlockSpec((1, cols), lambda i: (0, 0))],
            out_specs=(row_block, row_block),
            cost_estimate=pl.CostEstimate(flops=4 * rows * cols, bytes_accessed=8 * rows * cols, transcendentals=rows),
        )(h, ssq, gain.reshape(1, cols))

    row_spec = P(("dp", "tp"), "tp2")
    return jax.shard_map(local_step, mesh=mesh, in_specs=(P("dp", "tp"), P("tp", "tp2"), row_spec, P("tp2")),
                         out_specs=(row_spec, row_spec), check_vma=False)
```

time: 405 us -> 351 us (0.87)
  Pallas kernels: 386 us -> 348 us
  other arithmetic: 17.1 us -> 0 us
    pallas_call x1, Pallas kernels: 386 us -> 336 us  [local_step(): pl.pallas_call(functools.partial(kernel, ny, chips), out_shape=(jax.Shape...]
    convert_element_type x1 -> x0, other arithmetic: 16.3 us -> none  [local_step(): return (hidden.astype(jnp.bfloat16), normed.astype(jnp.bfloat16))]
    pallas_call x0 -> x1, Pallas kernels: none -> 12 us  [local_step(): pl.pallas_call(functools.partial(norm_kernel, cols * ny), grid=(rows // s...]
where the time goes in v2:
time: 351 us; the launch traced here: 349 us
  Pallas kernels  348 us (99%)
    pallas_call x1, Pallas kernels, local_step(): pl.pallas_call(functools.partial(kernel, ny, chips), out_shape=(jax.Shape...  336 us
    pallas_call x1, Pallas kernels, local_step(): pl.pallas_call(functools.partial(norm_kernel, cols * ny), grid=(rows // s...  12 us

profile of v2, /device:TPU:96, one launch (start us, length us, event | category | flops | bytes accessed | tf_op | source)
XLA Modules:
  0.0 348.8 jit_solution(7158244977210696425)
XLA Ops:
  0.6 336.1 %shard_map.59 = (f32[1024,3072]{1,0:T(8,128)}, f32[8,1024]{1,0:T(8,128)}, bf16[3,11,1536,256]{3,2,1,0:T(8,128)(2,1)}) custom-call(bf16[8192,1536]{1,0:T(8,128)(2,1)} %a.1, bf16[1536,3072]{1,0:T(8,128)(2,1)} %w.1, bf16[1024,3072]{1,0:T(8,128)(2,1)} %r.1), custom_call_target="tpu_custom_call" | custom-call | flops 77309411328 | bytes 75497472 | tf_op jit(solution)/shard_map/pallas_call | solution.py:418
  336.7 12.0 %shard_map.60 = (bf16[1024,3072]{1,0:T(8,128)(2,1)}, bf16[1024,3072]{1,0:T(8,128)(2,1)}) custom-call(f32[1024,3072]{1,0:T(8,128)} %get-tuple-element.4.h, f32[8,1024]{1,0:T(8,128)} %get-tuple-element.5.ssq, f32[1,3072]{1,0:T(1,128)} %bitcast.1), custom_call_target="tpu_custom_call" | custom-call | flops 12582912 | bytes 25165824 | tf_op jit(solution)/shard_map/pallas_call | solution.py:457
